TPU v7x, 32 devices: a whole 2x2x4 slice. The times are simulated.
32 devices in a mesh: dp: 8 (over z, y), mp: 4 (over x, core).
Axes of the slice: x: 2, y: 2, z: 4, core: 2. Of those that a mesh axis runs over, the one named last changes fastest.
Arguments:
- features: bfloat16 [3, 512, 16384], P(None, 'mp', 'dp'), may hold values from -6 to 6
- weights: bfloat16 [11, 512, 512], P(None, 'mp'), may hold values from -0.25 to 0.25
- sample_owner: int32 [3, 16384, 1], P(None, 'dp'), may hold values from 0 to 7; in each aligned block of 2048 rows (0 to 2047, 2048 to 4095, ..., all dimensions but the last counted through in order) at most 512 rows name the same one
- sample_row: int32 [3, 16384], P(None, 'dp'), may hold values from 0 to 2047
- edge_src: int32 [8, 16384], P(None, 'dp'), may hold values from 0 to 2047
- edge_dst: int32 [8, 16384], P(None, 'dp'), may hold values from 0 to 127
- edge_count: int32 [8, 8], P(None, 'dp'), may hold values from 128 to 2048
Outputs:
- updated: bfloat16 [3, 512, 1024], P(None, 'mp', 'dp')
Inputs may be any that keep to these rules, and one draw needn't show every extreme that they name: `sample_owner`: among the 2048 entries of one node type in one block no owner appears more than 512 times; some owner appears exactly 512 times in some blocks.
All inputs are finite; a program needn't handle non-finite values.
Results may differ from a plain program's by a relative error of at most 0.0064.
Values may be sent and summed in bfloat16 or wider, within the bound.
A program may use at most 64 MiB of HBM per device.

v0:
```python
import math

import jax
import jax.numpy as jnp
from jax import lax
from jax.sharding import PartitionSpec as P

RELS = 8
SEEDS = 128


RELATION_SOURCE = (0, 1, 0, 1, 2, 0, 2, 1)
MATRIX_TARGET = (1, 0, 0, 2, 1, 2, 0, 1, 0, 1, 2)


def pick_columns(table, index):
    count = index.shape[0]
    block_size = math.gcd(count, 512)
    row_ids = jnp.arange(table.shape[1], dtype=jnp.int32)[:, None]

    def one_block(block):
        chosen = (row_ids == block[None, :]).astype(jnp.bfloat16)
        return jnp.dot(table, chosen, preferred_element_type=jnp.float32).astype(jnp.bfloat16)

    picked = lax.map(one_block, index.reshape(count // block_size, block_size))
    return picked.transpose(1, 0, 2).reshape(table.shape[0], count)


def serve_kind(kind_table, requested):
    picked = pick_columns(kind_table, requested.reshape(-1))
    picked = picked.reshape(kind_table.shape[0], requested.shape[0], requested.shape[1])
    return lax.all_to_all(picked, "dp", split_axis=1, concat_axis=1, tiled=True)


def contract_first(left, right):
    return lax.dot_general(
        left, right, (((0,), (0,)), ((), ())), preferred_element_type=jnp.float32
    )


def per_device(features, weights, sample_owner, sample_row, edge_src, edge_dst, edge_count):
    groups = lax.axis_size("dp")
    node_kinds = features.shape[0]
    width_here = features.shape[1]
    sampled = sample_row.shape[1]
    capacity = 2 * sampled // groups
    owners = sample_owner[:, :, 0]
    owner_hot = (owners[:, :, None] == jnp.arange(groups, dtype=jnp.int32)[None, None, :]).astype(
        jnp.float32
    )
    block_size = math.gcd(sampled, 512)
    blocks = owner_hot.reshape(node_kinds, sampled // block_size, block_size, groups)
    block_ids = jnp.arange(block_size, dtype=jnp.int32)
    lower = (block_ids[:, None] >= block_ids[None, :]).astype(jnp.float32)
    within = jnp.einsum("ij,tbjo->tbio", lower, blocks, precision=lax.Precision.HIGHEST)
    totals = jnp.sum(blocks, axis=2)
    before = jnp.cumsum(totals, axis=1) - totals
    inclusive = (within + before[:, :, None, :]).reshape(node_kinds, sampled, groups)
    slot_rank = jnp.sum((inclusive - 1.0) * owner_hot, axis=2).astype(jnp.int32)
    position = owners * capacity + slot_rank
    rank_hot = (
        slot_rank[:, :, None] == jnp.arange(capacity, dtype=jnp.int32)[None, None, :]
    ).astype(jnp.float32)
    weighted_owner = owner_hot * sample_row[:, :, None].astype(jnp.float32)
    requests = jnp.einsum(
        "tio,tik->tok", weighted_owner, rank_hot, precision=lax.Precision.HIGHEST
    ).astype(jnp.int32)
    fetched_parts = []
    for node_kind in range(node_kinds):
        fetched_parts.append(
            serve_kind(
                features[node_kind],
                lax.all_to_all(requests[node_kind], "dp", split_axis=0, concat_axis=0, tiled=True),
            )
        )
    fetched = jnp.stack(fetched_parts)
    fetched = fetched.reshape(node_kinds, width_here, groups * capacity)
    gathered = jnp.stack(
        [pick_columns(fetched[node_kind], position[node_kind]) for node_kind in range(node_kinds)]
    )
    edge_total = edge_src.shape[1]
    seed_ids = jnp.arange(SEEDS, dtype=jnp.int32)[:, None]
    slot_ids = jnp.arange(edge_total, dtype=jnp.int32)
    messages = []
    for relation in range(RELS):
        live_edge = slot_ids < edge_count[relation, 0]
        target = jnp.where(live_edge, edge_dst[relation], -1)
        dst_hot = (seed_ids == target[None, :]).astype(jnp.bfloat16)
        sources = pick_columns(gathered[RELATION_SOURCE[relation]], edge_src[relation])
        summed = lax.dot_general(
            sources, dst_hot, (((1,), (1,)), ((), ())), preferred_element_type=jnp.float32
        )
        degree = jnp.sum(dst_hot, axis=1, dtype=jnp.float32)
        messages.append((summed / jnp.maximum(degree, 1.0)[None, :]).astype(jnp.bfloat16))
    for node_kind in range(node_kinds):
        messages.append(gathered[node_kind, :, :SEEDS])
    stacked = jnp.stack(messages)
    full_width = weights.shape[2]
    partial_sums = [jnp.zeros((full_width, SEEDS), jnp.float32) for node_kind in range(node_kinds)]
    for matrix in range(stacked.shape[0]):
        partial_sums[MATRIX_TARGET[matrix]] = partial_sums[MATRIX_TARGET[matrix]] + contract_first(
            weights[matrix], stacked[matrix]
        )
    typed = lax.psum_scatter(jnp.stack(partial_sums), "mp", scatter_dimension=1, tiled=True)
    return jax.nn.relu(typed).astype(jnp.bfloat16)


def solution(mesh):
    return jax.shard_map(
        per_device,
        mesh=mesh,
        in_specs=(
            P(None, "mp", "dp"),
            P(None, "mp", None),
            P(None, "dp", None),
            P(None, "dp"),
            P(None, "dp"),
            P(None, "dp"),
            P(None, "dp"),
        ),
        out_specs=P(None, "mp", "dp"),
        check_vma=False,
    )
```

profile of v0, /device:TPU:1, one launch (start us, length us, event | category | flops | bytes accessed | tf_op | source)
XLA Modules:
  0.0 244.8 jit_solution(14992279231206325996)
XLA Ops:
  9.4 4.3 %fusion.227 = s32[3,8,512]{2,1,0:T(8,128)S(1)} fusion(s32[3,2048]{1,0:T(4,128)S(1)} %bitcast.375, f32[3,2048]{1,0:T(4,128)S(1)} %convert_element_type.199, s32[3,2048]{1,0:T(4,128)S(1)} %bitcast.394), kind=kOutput, calls=%fused_computation.161 | convolution fusion | flops 305246208 | bytes 122880 | tf_op jit(solution)/shard_map/tio,tik->tok/dot_general | solution.py:65
  14.4 6.4 %all-to-all-start = ((s32[8,1,512]{2,1,0:T(1,128)}), s32[8,1,512]{2,1,0:T(1,128)S(1)}, u32[]{:S(2)}, u32[]{:S(2)}) async-start(s32[8,1,512]{2,1,0:T(1,128)} %copy.32), calls=%async_computation | async-start | bytes 32768 | tf_op jit(solution)/shard_map/all_to_all | solution.py:73
  21.5 5.1 %compare_select_fusion.5 = (s32[1,2048]{1,0:T(1,128)S(1)}, s32[1,2048]{1,0:T(1,128)S(1)}, s32[1,2048]{1,0:T(1,128)S(1)}, s32[1,2048]{1,0:T(1,128)S(1)}, s32[1,20...) fusion(s32[8,2048]{1,0:T(8,128)S(1)} %copy-done.14, s32[]{:T(128)} %bitcast.33, ...), kind=kLoop, calls=%fused_computation.252 | loop fusion | flops 32768 | bytes 131104 | tf_op jit(solution)/shard_map/jit(_where)/select_n | solution.py:87
  29.0 5.4 %all-to-all-start.2 = ((s32[8,1,512]{2,1,0:T(1,128)}), s32[8,1,512]{2,1,0:T(1,128)S(1)}, u32[]{:S(2)}, u32[]{:S(2)}) async-start(s32[8,1,512]{2,1,0:T(1,128)} %copy.35), calls=%async_computation.2 | async-start | bytes 32768 | tf_op jit(solution)/shard_map/all_to_all | solution.py:73
  35.4 4.4 %all-to-all-done.2 = s32[8,1,512]{2,1,0:T(1,128)S(1)} async-done(((s32[8,1,512]{2,1,0:T(1,128)}), s32[8,1,512]{2,1,0:T(1,128)S(1)}, u32[]{:S(2)}, u32[]{:S(2)}) %all-to-all-start.2) | async-done | bytes 16416 | tf_op jit(solution)/shard_map/all_to_all | solution.py:73
  44.3 11.4 %while.154 = (s32[]{:T(128)}, bf16[8,128,512]{1,2,0:T(8,128)(2,1)}, s32[8,512]{1,0:T(8,128)S(1)}, bf16[128,2048]{1,0:T(8,128)(2,1)S(1)}, s32[]{:T(128)}) while((s32[]{:T(128)}, bf16[8,128,512]{1,2,0:T(8,128)(2,1)}, s32[8,512]{1,0:T(8,128)S(1)}, bf16[128,2048]{1,0:T(8,128)(2,1)S(1)}, s32[]{:T(128)}) %tuple.315), condition=%wide.region_4.5_spmd.clone, body=%wide.region_3.4_spmd.clone.sunk | while | flops 270598144 | bytes 662081 | solution.py:25
  55.7 5.4 %all-to-all-start.1 = ((bf16[128,8,512]{0,2,1:T(8,128)(2,1)}), bf16[128,8,512]{0,2,1:T(8,128)(2,1)S(1)}, u32[]{:S(2)}, u32[]{:S(2)}) async-start(bf16[128,8,512]{0,2,1:T(8,128)(2,1)} %bitcast.5), calls=%async_computation.1 | async-start | bytes 2097152 | tf_op jit(solution)/shard_map/all_to_all | solution.py:32
  62.2 11.3 %while.157 = (s32[]{:T(128)}, bf16[8,128,512]{1,2,0:T(8,128)(2,1)}, s32[8,512]{1,0:T(8,128)S(1)}, bf16[128,2048]{1,0:T(8,128)(2,1)S(1)}, s32[]{:T(128)}) while((s32[]{:T(128)}, bf16[8,128,512]{1,2,0:T(8,128)(2,1)}, s32[8,512]{1,0:T(8,128)S(1)}, bf16[128,2048]{1,0:T(8,128)(2,1)S(1)}, s32[]{:T(128)}) %tuple.314), condition=%wide.region_11.12_spmd.clone, body=%wide.region_10.11_spmd.clone.sunk | while | flops 270598144 | bytes 662081 | solution.py:25
  73.6 11.4 %all-to-all-done.1 = bf16[128,8,512]{0,2,1:T(8,128)(2,1)S(1)} async-done(((bf16[128,8,512]{0,2,1:T(8,128)(2,1)}), bf16[128,8,512]{0,2,1:T(8,128)(2,1)S(1)}, u32[]{:S(2)}, u32[]{:S(2)}) %all-to-all-start.1) | async-done | bytes 1048608 | tf_op jit(solution)/shard_map/all_to_all | solution.py:32
  85.0 4.9 %all-to-all-start.3 = ((bf16[128,8,512]{0,2,1:T(8,128)(2,1)}), bf16[128,8,512]{0,2,1:T(8,128)(2,1)S(1)}, u32[]{:S(2)}, u32[]{:S(2)}) async-start(bf16[128,8,512]{0,2,1:T(8,128)(2,1)} %bitcast.16), calls=%async_computation.3 | async-start | bytes 2097152 | tf_op jit(solution)/shard_map/all_to_all | solution.py:32
  91.0 11.3 %while.160 = (s32[]{:T(128)}, bf16[8,128,512]{1,2,0:T(8,128)(2,1)}, s32[8,512]{1,0:T(8,128)S(1)}, bf16[128,2048]{1,0:T(8,128)(2,1)S(1)}, s32[]{:T(128)}) while((s32[]{:T(128)}, bf16[8,128,512]{1,2,0:T(8,128)(2,1)}, s32[8,512]{1,0:T(8,128)S(1)}, bf16[128,2048]{1,0:T(8,128)(2,1)S(1)}, s32[]{:T(128)}) %tuple.313), condition=%wide.region_18.19_spmd.clone, body=%wide.region_17.18_spmd.clone.sunk | while | flops 270598144 | bytes 662081 | solution.py:25
  103.7 10.5 %while.155 = (s32[]{:T(128)}, bf16[4,128,512]{1,2,0:T(8,128)(2,1)S(1)}, s32[4,512]{1,0:T(4,128)S(1)}, bf16[128,4096]{1,0:T(8,128)(2,1)}, s32[]{:T(128)}) while((s32[]{:T(128)}, bf16[4,128,512]{1,2,0:T(8,128)(2,1)S(1)}, s32[4,512]{1,0:T(4,128)S(1)}, bf16[128,4096]{1,0:T(8,128)(2,1)}, s32[]{:T(128)}) %tuple.267), condition=%wide.region_6.7_spmd.clone, body=%wide.region_5.6_spmd.clone.sunk | while | flops 541130752 | bytes 1185861 | solution.py:25
  115.2 5.4 %all-to-all-start.5 = ((bf16[128,8,512]{0,2,1:T(8,128)(2,1)}), bf16[128,8,512]{0,2,1:T(8,128)(2,1)S(1)}, u32[]{:S(2)}, u32[]{:S(2)}) async-start(bf16[128,8,512]{0,2,1:T(8,128)(2,1)} %bitcast.27), calls=%async_computation.5 | async-start | bytes 2097152 | tf_op jit(solution)/shard_map/all_to_all | solution.py:32
  122.3 10.5 %while.158 = (s32[]{:T(128)}, bf16[4,128,512]{1,2,0:T(8,128)(2,1)S(1)}, s32[4,512]{1,0:T(4,128)S(1)}, bf16[128,4096]{1,0:T(8,128)(2,1)}, s32[]{:T(128)}) while((s32[]{:T(128)}, bf16[4,128,512]{1,2,0:T(8,128)(2,1)S(1)}, s32[4,512]{1,0:T(4,128)S(1)}, bf16[128,4096]{1,0:T(8,128)(2,1)}, s32[]{:T(128)}) %tuple.276), condition=%wide.region_13.14_spmd.clone, body=%wide.region_12.13_spmd.clone.sunk | while | flops 541130752 | bytes 1185861 | solution.py:25
  132.9 3.4 %while.156 = (s32[]{:T(128)}, bf16[4,128,512]{1,2,0:T(8,128)(2,1)S(1)}, s32[4,512]{1,0:T(4,128)S(1)}, bf16[128,2048]{1,0:T(8,128)(2,1)S(1)}, s32[]{:T(128)}) while((s32[]{:T(128)}, bf16[4,128,512]{1,2,0:T(8,128)(2,1)S(1)}, s32[4,512]{1,0:T(4,128)S(1)}, bf16[128,2048]{1,0:T(8,128)(2,1)S(1)}, s32[]{:T(128)}) %tuple.308), condition=%wide.region_8.9_spmd.clone, body=%wide.region_7.8_spmd.clone.sunk | while | flops 270598144 | bytes 661573 | solution.py:25
  137.4 7.6 %while.159 = (s32[]{:T(128)}, bf16[4,128,512]{1,2,0:T(8,128)(2,1)S(1)}, s32[4,512]{1,0:T(4,128)S(1)}, bf16[128,2048]{1,0:T(8,128)(2,1)}, s32[]{:T(128)}) while((s32[]{:T(128)}, bf16[4,128,512]{1,2,0:T(8,128)(2,1)S(1)}, s32[4,512]{1,0:T(4,128)S(1)}, bf16[128,2048]{1,0:T(8,128)(2,1)}, s32[]{:T(128)}) %tuple.300), condition=%wide.region_15.16_spmd.clone, body=%wide.region_14.15_spmd.clone.sunk | while | flops 270598144 | bytes 661573 | solution.py:25
  146.4 5.6 %while.161 = (s32[]{:T(128)}, bf16[4,128,512]{1,2,0:T(8,128)(2,1)S(1)}, s32[4,512]{1,0:T(4,128)S(1)}, bf16[128,4096]{1,0:T(8,128)(2,1)S(1)}, s32[]{:T(128)}) while((s32[]{:T(128)}, bf16[4,128,512]{1,2,0:T(8,128)(2,1)S(1)}, s32[4,512]{1,0:T(4,128)S(1)}, bf16[128,4096]{1,0:T(8,128)(2,1)S(1)}, s32[]{:T(128)}) %tuple.285), condition=%wide.region_20.21_spmd.clone, body=%wide.region_19.20_spmd.clone.sunk | while | flops 541130752 | bytes 1185861 | solution.py:25
  153.1 7.6 %while.162 = (s32[]{:T(128)}, bf16[4,128,512]{1,2,0:T(8,128)(2,1)S(1)}, s32[4,512]{1,0:T(4,128)S(1)}, bf16[128,2048]{1,0:T(8,128)(2,1)}, s32[]{:T(128)}) while((s32[]{:T(128)}, bf16[4,128,512]{1,2,0:T(8,128)(2,1)S(1)}, s32[4,512]{1,0:T(4,128)S(1)}, bf16[128,2048]{1,0:T(8,128)(2,1)}, s32[]{:T(128)}) %tuple.303), condition=%wide.region_22.23_spmd.clone, body=%wide.region_21.22_spmd.clone.sunk | while | flops 270598144 | bytes 661573 | solution.py:25
  161.5 3.4 %while.163 = (s32[]{:T(128)}, bf16[4,128,512]{1,2,0:T(8,128)(2,1)S(1)}, s32[4,512]{1,0:T(4,128)S(1)}, bf16[128,2048]{1,0:T(8,128)(2,1)S(1)}, s32[]{:T(128)}) while((s32[]{:T(128)}, bf16[4,128,512]{1,2,0:T(8,128)(2,1)S(1)}, s32[4,512]{1,0:T(4,128)S(1)}, bf16[128,2048]{1,0:T(8,128)(2,1)S(1)}, s32[]{:T(128)}) %tuple.311), condition=%wide.region_25.26_spmd.clone, body=%wide.region_24.25_spmd.clone.sunk | while | flops 270598144 | bytes 661573 | solution.py:25
  165.7 7.5 %while.164 = (s32[]{:T(128)}, bf16[4,128,512]{1,2,0:T(8,128)(2,1)S(1)}, s32[4,512]{1,0:T(4,128)S(1)}, bf16[128,2048]{1,0:T(8,128)(2,1)}, s32[]{:T(128)}) while((s32[]{:T(128)}, bf16[4,128,512]{1,2,0:T(8,128)(2,1)S(1)}, s32[4,512]{1,0:T(4,128)S(1)}, bf16[128,2048]{1,0:T(8,128)(2,1)}, s32[]{:T(128)}) %tuple.291), condition=%wide.region_28.29_spmd.clone, body=%wide.region_27.28_spmd.clone.sunk | while | flops 270598144 | bytes 661573 | solution.py:25
  174.1 3.4 %while.165 = (s32[]{:T(128)}, bf16[4,128,512]{1,2,0:T(8,128)(2,1)S(1)}, s32[4,512]{1,0:T(4,128)S(1)}, bf16[128,2048]{1,0:T(8,128)(2,1)S(1)}, s32[]{:T(128)}) while((s32[]{:T(128)}, bf16[4,128,512]{1,2,0:T(8,128)(2,1)S(1)}, s32[4,512]{1,0:T(4,128)S(1)}, bf16[128,2048]{1,0:T(8,128)(2,1)S(1)}, s32[]{:T(128)}) %tuple.309), condition=%wide.region_31.32_spmd.clone, body=%wide.region_30.31_spmd.clone.sunk | while | flops 270598144 | bytes 661573 | solution.py:25
  178.4 5.7 %while.166 = (s32[]{:T(128)}, bf16[4,128,512]{1,2,0:T(8,128)(2,1)}, s32[4,512]{1,0:T(4,128)S(1)}, bf16[128,2048]{1,0:T(8,128)(2,1)S(1)}, s32[]{:T(128)}) while((s32[]{:T(128)}, bf16[4,128,512]{1,2,0:T(8,128)(2,1)}, s32[4,512]{1,0:T(4,128)S(1)}, bf16[128,2048]{1,0:T(8,128)(2,1)S(1)}, s32[]{:T(128)}) %tuple.310), condition=%wide.region_34.35_spmd.clone, body=%wide.region_33.34_spmd.clone.sunk | while | flops 270598144 | bytes 662081 | solution.py:25
  184.2 7.9 %while.167 = (s32[]{:T(128)}, bf16[4,128,512]{1,2,0:T(8,128)(2,1)S(1)}, s32[4,512]{1,0:T(4,128)S(1)}, bf16[128,2048]{1,0:T(8,128)(2,1)}, s32[]{:T(128)}) while((s32[]{:T(128)}, bf16[4,128,512]{1,2,0:T(8,128)(2,1)S(1)}, s32[4,512]{1,0:T(4,128)S(1)}, bf16[128,2048]{1,0:T(8,128)(2,1)}, s32[]{:T(128)}) %tuple.312), condition=%wide.region_37.38_spmd.clone, body=%wide.region_36.37_spmd.clone.sunk | while | flops 270598144 | bytes 661573 | solution.py:25
  210.4 25.8 %reduce-scatter.2.cloned.1.call-done = f32[3,128,128]{1,2,0:T(8,128)} async-done(((f32[3,512,128]{1,2,0:T(8,128)}), f32[3,128,128]{1,2,0:T(8,128)}) %reduce-scatter.2.cloned.1.call-update) | async-done | bytes 196624 | tf_op jit(solution)/shard_map/reduce_scatter | solution.py:104
  (259 shorter events, 151.0 us)
Async XLA Ops:
  9.4 11.4 %copy-start.13 = (s32[3,2048,1]{1,2,0:T(1,128)S(1)}, s32[3,2048,1]{1,2,0:T(1,128)}, u32[]{:S(2)}) copy-start(s32[3,2048,1]{1,2,0:T(1,128)} %param.37) | copy-start | bytes 73732
  9.4 11.4 %copy-start.16 = (s32[8,1]{0,1:T(1,128)S(1)}, s32[8,1]{0,1:T(1,128)}, u32[]{:S(2)}) copy-start(s32[8,1]{0,1:T(1,128)} %param.41) | copy-start | bytes 100
  9.4 12.1 %copy-start.14 = (s32[8,2048]{1,0:T(8,128)S(1)}, s32[8,2048]{1,0:T(8,128)}, u32[]{:S(2)}) copy-start(s32[8,2048]{1,0:T(8,128)} %param.40) | copy-start | bytes 196612
  9.4 17.4 %copy-start = (bf16[3,128,2048]{2,1,0:T(8,128)(2,1)S(1)}, bf16[3,128,2048]{2,1,0:T(8,128)(2,1)}, u32[]{:S(2)}) copy-start(bf16[3,128,2048]{2,1,0:T(8,128)(2,1)} %param.35) | copy-start | bytes 4718596
  14.4 14.6 %all-to-all-start = ((s32[8,1,512]{2,1,0:T(1,128)}), s32[8,1,512]{2,1,0:T(1,128)S(1)}, u32[]{:S(2)}, u32[]{:S(2)}) async-start(s32[8,1,512]{2,1,0:T(1,128)} %copy.32), calls=%async_computation | async-start | bytes 32768 | tf_op jit(solution)/shard_map/all_to_all | solution.py:73
  26.8 7.6 %copy-start.15 = (s32[8,2048]{1,0:T(8,128)S(1)}, s32[8,2048]{1,0:T(8,128)}, u32[]{:S(2)}) copy-start(s32[8,2048]{1,0:T(8,128)} %param.39) | copy-start | bytes 196612
  29.0 10.9 %all-to-all-start.2 = ((s32[8,1,512]{2,1,0:T(1,128)}), s32[8,1,512]{2,1,0:T(1,128)S(1)}, u32[]{:S(2)}, u32[]{:S(2)}) async-start(s32[8,1,512]{2,1,0:T(1,128)} %copy.35), calls=%async_computation.2 | async-start | bytes 32768 | tf_op jit(solution)/shard_map/all_to_all | solution.py:73
  39.8 15.8 %all-to-all-start.4 = ((s32[8,1,512]{2,1,0:T(1,128)}), s32[8,1,512]{2,1,0:T(1,128)S(1)}, u32[]{:S(2)}, u32[]{:S(2)}) async-start(s32[8,1,512]{2,1,0:T(1,128)} %copy.38), calls=%async_computation.4 | async-start | bytes 32768 | tf_op jit(solution)/shard_map/all_to_all | solution.py:73
  55.7 29.3 %all-to-all-start.1 = ((bf16[128,8,512]{0,2,1:T(8,128)(2,1)}), bf16[128,8,512]{0,2,1:T(8,128)(2,1)S(1)}, u32[]{:S(2)}, u32[]{:S(2)}) async-start(bf16[128,8,512]{0,2,1:T(8,128)(2,1)} %bitcast.5), calls=%async_computation.1 | async-start | bytes 2097152 | tf_op jit(solution)/shard_map/all_to_all | solution.py:32
  85.0 30.2 %all-to-all-start.3 = ((bf16[128,8,512]{0,2,1:T(8,128)(2,1)}), bf16[128,8,512]{0,2,1:T(8,128)(2,1)S(1)}, u32[]{:S(2)}, u32[]{:S(2)}) async-start(bf16[128,8,512]{0,2,1:T(8,128)(2,1)} %bitcast.16), calls=%async_computation.3 | async-start | bytes 2097152 | tf_op jit(solution)/shard_map/all_to_all | solution.py:32
  115.2 29.8 %all-to-all-start.5 = ((bf16[128,8,512]{0,2,1:T(8,128)(2,1)}), bf16[128,8,512]{0,2,1:T(8,128)(2,1)S(1)}, u32[]{:S(2)}, u32[]{:S(2)}) async-start(bf16[128,8,512]{0,2,1:T(8,128)(2,1)} %bitcast.27), calls=%async_computation.5 | async-start | bytes 2097152 | tf_op jit(solution)/shard_map/all_to_all | solution.py:32
  120.7 115.6 %reduce-scatter.2.cloned.1.call-start = ((), (), s32[]{:S(2)}) async-start(), calls=%async_computation.7 | async-start | bytes 983040 | tf_op jit(solution)/shard_map/reduce_scatter | solution.py:104
  122.3 10.6 %copy-start.10 = (bf16[128,2048]{1,0:T(8,128)(2,1)S(1)}, bf16[128,2048]{1,0:T(8,128)(2,1)}, u32[]{:S(2)}) copy-start(bf16[128,2048]{1,0:T(8,128)(2,1)} %copy.44) | copy-start | bytes 1572868
  136.3 1.1 copy-start.1
  145.0 0.8 copy-start.3
  153.1 7.7 %copy-start.12 = (bf16[128,2048]{1,0:T(8,128)(2,1)S(1)}, bf16[128,2048]{1,0:T(8,128)(2,1)}, u32[]{:S(2)}) copy-start(bf16[128,2048]{1,0:T(8,128)(2,1)} %get-tuple-element.1258) | copy-start | bytes 1572868
  160.7 0.8 copy-start.5
  164.9 0.8 copy-start.6
  165.0 8.4 %copy-start.11 = (bf16[128,2048]{1,0:T(8,128)(2,1)S(1)}, bf16[128,2048]{1,0:T(8,128)(2,1)}, u32[]{:S(2)}) copy-start(bf16[128,2048]{1,0:T(8,128)(2,1)} %copy.44) | copy-start | bytes 1572868
  173.3 0.8 copy-start.8
  177.4 1.0 copy-start.9
  184.1 7.9 %copy-start.2 = (bf16[4,128,512]{1,2,0:T(8,128)(2,1)S(1)}, bf16[4,128,512]{1,2,0:T(8,128)(2,1)}, u32[]{:S(2)}) copy-start(bf16[4,128,512]{1,2,0:T(8,128)(2,1)} %copy-done.1) | copy-start | bytes 1572868
  184.2 10.1 %copy-start.4 = (bf16[4,128,512]{1,2,0:T(8,128)(2,1)S(1)}, bf16[4,128,512]{1,2,0:T(8,128)(2,1)}, u32[]{:S(2)}) copy-start(bf16[4,128,512]{1,2,0:T(8,128)(2,1)} %copy-done.3) | copy-start | bytes 1572868
  194.2 5.2 %copy-start.7 = (bf16[4,128,512]{1,2,0:T(8,128)(2,1)S(1)}, bf16[4,128,512]{1,2,0:T(8,128)(2,1)}, u32[]{:S(2)}) copy-start(bf16[4,128,512]{1,2,0:T(8,128)(2,1)} %copy-done.6) | copy-start | bytes 1572868
Sparse Core Ops, SparseCore 0:
  210.6 25.6 reduce-scatter.1
where the time goes:
time: 248 us; the launch traced here: 245 us
  matrix products  127 us (51%)
  waiting for transfers between devices  41.7 us (17%)
  starting transfers between devices  31.1 us (13%)
  local copies, waits for them, and re-layouts  19.3 us (8%)
  between operations  14 us (6%)
  other arithmetic  10.3 us (4%)
    dot_general x68, matrix products, one_block(): jnp.dot(table, chosen, preferred_element_type=jnp.float32)  105 us
    reduce_scatter x1, waiting for transfers between devices, per_device(): lax.psum_scatter(jnp.stack(partial_sums), 'mp', scatter_dimension=1, tile...  25.8 us
    dot_general x11, matrix products, contract_first(): lax.dot_general(left, right, (((0,), (0,)), ((), ())), preferred_element_...  17.3 us
    all_to_all x3, starting transfers between devices, serve_kind(): return lax.all_to_all(picked, 'dp', split_axis=1, concat_axis=1, tiled=True)  15.7 us
    all_to_all x3, starting transfers between devices, per_device(): lax.all_to_all(requests[node_kind], 'dp', split_axis=0, concat_axis=0, ti...  15.1 us
    all_to_all x3, waiting for transfers between devices, serve_kind(): return lax.all_to_all(picked, 'dp', split_axis=1, concat_axis=1, tiled=True)  11.4 us
    another operation x14, local copies, waits for them, and re-layouts  5.08 us
    select_n x1, other arithmetic, per_device(): target = jnp.where(live_edge, edge_dst[relation], -1)  5.06 us
  transfers between devices with their start and end apart: 7, of which 3 were waited for; matrix products, arithmetic and copies ran while one was open for 34% of the time, Pallas kernels for 0%

commit v1 on v0

v1 whole, which is shorter than its diff:
```python
import functools

import jax
import jax.numpy as jnp
from jax import lax
from jax.experimental import pallas as pl
from jax.experimental.pallas import tpu as pltpu
from jax.sharding import PartitionSpec as P

SEEDS = 128
RELATION_SOURCE = (0, 1, 0, 1, 2, 0, 2, 1)
MATRIX_TARGET = (1, 0, 0, 2, 1, 2, 0, 1, 0, 1, 2)
RELS = len(RELATION_SOURCE)
KINDS = 3
MATS = RELS + KINDS
SLOTS = tuple(
    tuple([r for r in range(RELS) if RELATION_SOURCE[r] == k] + [RELS + k]) for k in range(KINDS)
)
ORDER = tuple(m for group in SLOTS for m in group)
STARTS = tuple(sum(len(group) for group in SLOTS[:k]) for k in range(KINDS))
HALVES = 2
STEP = 256
MESH = pl.DeviceIdType.MESH
NT = (((1,), (1,)), ((), ()))
TN = (((0,), (0,)), ((), ()))


def log2(n):
    return n.bit_length() - 1


def kernel(groups, shares, features, weights, owner, row, src, dst, count, out,
           iota, tab, req_send, req_recv, pos, edges, send, recv, adj, deg, part,
           part_send, part_recv, typed, typed_send, typed_recv,
           req_ss, req_rs, idx_ss, idx_rs, row_ss, row_rs, part_ss, part_rs, typed_ss, typed_rs):
    kinds, feat, rows = features.shape
    sampled = owner.shape[1]
    edge_total = src.shape[1]
    cap = req_send.shape[2]
    low = tab.shape[2]
    high = rows // low
    s_high = sampled // low
    side = groups // HALVES
    g = lax.axis_index("dp")
    m = lax.axis_index("mp")
    half = g // side
    q = lax.rem(g, side)
    f32, bf16, i32 = jnp.float32, jnp.bfloat16, jnp.int32

    def one_hot(index, size):
        n = index.shape[1]
        pieces = []
        for base in range(0, size, STEP):
            span = min(STEP, size - base)
            local = index - base
            local = jnp.where((local >= 0) & (local < span), local, -1).astype(f32).astype(bf16)
            hit = iota[:span, :n] == local
            pieces.append(jnp.where(hit, jnp.ones((), bf16), jnp.zeros((), bf16)))
        return pieces[0] if len(pieces) == 1 else jnp.concatenate(pieces, axis=0)

    barrier = pltpu.get_barrier_semaphore()
    for d in range(1, groups):
        pl.semaphore_signal(barrier, inc=1, device_id={"dp": lax.rem(g + d, groups)}, device_id_type=MESH)
    for d in range(1, shares):
        pl.semaphore_signal(barrier, inc=1, device_id={"mp": lax.rem(m + d, shares)}, device_id_type=MESH)

    iota[...] = lax.broadcasted_iota(i32, iota.shape, 0).astype(f32).astype(bf16)
    tri = (lax.broadcasted_iota(i32, (STEP, STEP), 0) <= lax.broadcasted_iota(i32, (STEP, STEP), 1))
    tri = jnp.where(tri, 1.0, 0.0).astype(bf16)
    for k in range(kinds):
        owners = owner[k:k + 1, :]
        hot = jnp.where(lax.broadcasted_iota(i32, (groups, sampled), 0) == owners, 1.0, 0.0)
        carry = jnp.zeros((groups, 1), f32)
        ranks = []
        for base in range(0, sampled, STEP):
            piece = hot[:, base:base + STEP]
            upto = jnp.dot(piece.astype(bf16), tri, preferred_element_type=f32) + carry
            ranks.append(jnp.sum((upto - 1.0) * piece, axis=0, keepdims=True))
            carry = carry + jnp.sum(piece, axis=1, keepdims=True)
        rank = jnp.concatenate(ranks, axis=1).astype(i32)
        pos[half, k:k + 1, :] = owners * cap + rank
        wanted = row[k:k + 1, :]
        coarse = hot * (wanted >> 8).astype(f32)
        fine = hot * (wanted & 255).astype(f32)
        pair = jnp.concatenate([coarse, fine], axis=0).astype(bf16)
        listed = lax.dot_general(pair, one_hot(rank, cap), NT, preferred_element_type=f32)
        listed = (listed[:groups] * 256.0 + listed[groups:]).astype(i32)
        for o in range(groups):
            req_send[o, k:k + 1, :] = listed[o:o + 1]
    slots = lax.broadcasted_iota(i32, (RELS, edge_total), 1)
    edges[half] = jnp.where(slots < count[...], dst[...] * sampled + src[...], -1)

    pl.semaphore_wait(barrier, groups - 1 + shares - 1)
    asks = []
    for d in range(1, groups):
        to = lax.rem(g + d, groups)
        copy = pltpu.make_async_remote_copy(
            req_send.at[to], req_recv.at[g], req_ss.at[d], req_rs.at[d],
            device_id={"dp": to}, device_id_type=MESH)
        copy.start()
        asks.append(copy)
    hints = []
    for i in range(1, HALVES):
        to = lax.rem(half + i, HALVES) * side + q
        for n, ref in enumerate((pos, edges)):
            copy = pltpu.make_async_remote_copy(
                ref.at[half], ref.at[half], idx_ss.at[i, n], idx_rs.at[i, n],
                device_id={"dp": to}, device_id_type=MESH)
            copy.start()
            hints.append(copy)

    for k in range(kinds):
        for h in range(high):
            tab[k, h * feat:(h + 1) * feat, :] = features[k, :, h * low:(h + 1) * low]

    def build(i, lo_r, hi_r):
        block = lax.rem(half + i, HALVES)

        def one(r, _):
            packed = edges[block, pl.ds(r, 1), :]
            live = packed >= 0
            source = packed & (sampled - 1)
            left = one_hot(jnp.where(live, source & (low - 1), -1), low)
            column = (source >> log2(low)) * SEEDS + (packed >> log2(sampled))
            right = one_hot(jnp.where(live, column, -1), s_high * SEEDS)
            counts = lax.dot_general(left, right, NT, preferred_element_type=f32)
            adj[i, r] = counts.astype(bf16)
            total = jnp.sum(counts, axis=0, keepdims=True)
            seen = total[:, :SEEDS]
            for h in range(1, s_high):
                seen = seen + total[:, h * SEEDS:(h + 1) * SEEDS]
            deg[i, r] = jnp.broadcast_to(jnp.maximum(seen, 1.0), (8, SEEDS))
            return 0

        lax.fori_loop(lo_r, hi_r, one, 0)

    build(0, 0, 2)
    req_recv[g] = req_send[g]
    for copy in asks:
        copy.wait()

    def pick(k, block):
        wanted = req_recv[block, k:k + 1, :]
        found = jnp.dot(tab[k], one_hot(wanted & (low - 1), low), preferred_element_type=f32)
        bank = wanted >> log2(low)
        chosen = jnp.zeros((feat, cap), f32)
        for h in range(high):
            chosen = jnp.where(bank == h, found[h * feat:(h + 1) * feat], chosen)
        return chosen.astype(bf16)

    def row_copy(k, d, j):
        return pltpu.make_async_remote_copy(
            send.at[k, d, j], recv.at[k, j, q], row_ss.at[k, d, j], row_rs.at[k, d, j],
            device_id={"dp": half * side + lax.rem(q + d, side)}, device_id_type=MESH)

    for k in range(kinds):
        def serve(n, _, k=k):
            d, j = 1 + n // HALVES, lax.rem(n, HALVES)
            send[k, d, j] = pick(k, j * side + lax.rem(q + d, side))
            row_copy(k, d, j).start()
            return 0

        lax.fori_loop(0, (side - 1) * HALVES, serve, 0)
    for k in range(kinds):
        def keep(j, _, k=k):
            recv[k, j, q] = pick(k, j * side + q)
            return 0

        lax.fori_loop(0, HALVES, keep, 0)

    build(0, 2, RELS)
    for copy in hints:
        copy.wait()
    for i in range(1, HALVES):
        build(i, 0, RELS)

    replies = []
    for k in range(kinds):
        start, size = STARTS[k], len(SLOTS[k])

        def landed(n, _, k=k):
            row_copy(k, 1 + n // HALVES, lax.rem(n, HALVES)).wait()
            return 0

        lax.fori_loop(0, (side - 1) * HALVES, landed, 0)
        for i in reversed(range(HALVES)):
            block = lax.rem(half + i, HALVES)
            sums = [jnp.zeros((feat, SEEDS), f32) for _ in SLOTS[k][:-1]]
            stack = recv[k, block].reshape(side * feat, cap)
            for h in range(s_high):
                where = pos[block, k:k + 1, h * low:(h + 1) * low]
                found = jnp.dot(stack, one_hot(where & (cap - 1), cap), preferred_element_type=f32)
                holder = (where >> log2(cap)) - half * side
                chosen = jnp.zeros((feat, low), f32)
                for o in range(side):
                    chosen = jnp.where(holder == o, found[o * feat:(o + 1) * feat], chosen)
                chosen = chosen.astype(bf16)
                if h == 0:
                    own = chosen[:, :SEEDS].astype(f32)
                for n, r in enumerate(SLOTS[k][:-1]):
                    sums[n] = sums[n] + jnp.dot(
                        chosen, adj[i, r, :, h * SEEDS:(h + 1) * SEEDS], preferred_element_type=f32)
            values = [value / deg[i, r][:1] for value, r in zip(sums, SLOTS[k][:-1])] + [own]
            for n, value in enumerate(values):
                if i == 0:
                    part[start + n] = value
                else:
                    part_send[i, start + n] = value.astype(bf16)
            if i > 0:
                copy = pltpu.make_async_remote_copy(
                    part_send.at[i, pl.ds(start, size)], part_recv.at[i, pl.ds(start, size)],
                    part_ss.at[i, k], part_rs.at[i, k],
                    device_id={"dp": block * side + q}, device_id_type=MESH)
                copy.start()
                replies.append(copy)
    for copy in replies:
        copy.wait()

    sums = [jnp.zeros((SEEDS, weights.shape[2]), f32) for _ in range(kinds)]
    for n, matrix in enumerate(ORDER):
        message = part[n]
        for i in range(1, HALVES):
            message = message + part_recv[i, n].astype(f32)
        target = MATRIX_TARGET[matrix]
        sums[target] = sums[target] + lax.dot_general(
            message.astype(bf16), weights[matrix], TN, preferred_element_type=f32)
    width = typed.shape[3]
    for t in range(kinds):
        for p in range(shares):
            piece = sums[t][:, p * width:(p + 1) * width]
            typed[p, t] = piece
            typed_send[p, t] = piece.astype(bf16)
    last = []
    for d in range(1, shares):
        to = lax.rem(m + d, shares)
        copy = pltpu.make_async_remote_copy(
            typed_send.at[to], typed_recv.at[d], typed_ss.at[d], typed_rs.at[d],
            device_id={"mp": to}, device_id_type=MESH)
        copy.start()
        last.append(copy)
    for copy in last:
        copy.wait()
    for t in range(kinds):
        total = typed[m, t]
        for d in range(1, shares):
            total = total + typed_recv[d, t].astype(f32)
        out[t] = jnp.maximum(total, 0.0).T.astype(bf16)


def per_device(features, weights, sample_owner, sample_row, edge_src, edge_dst, edge_count):
    groups, shares = lax.axis_size("dp"), lax.axis_size("mp")
    kinds, feat, rows = features.shape
    sampled, edge_total = sample_row.shape[1], edge_src.shape[1]
    cap = 2 * sampled // groups
    low = min(512, rows, sampled)
    side = groups // HALVES
    width = weights.shape[2] // shares
    bf16, f32, i32 = jnp.bfloat16, jnp.float32, jnp.int32
    vmem = pl.BlockSpec(memory_space=pltpu.VMEM)
    dma = pltpu.SemaphoreType.DMA
    return pl.pallas_call(
        functools.partial(kernel, groups, shares),
        out_shape=jax.ShapeDtypeStruct((kinds, width, SEEDS), bf16),
        in_specs=[vmem] * 7,
        out_specs=vmem,
        scratch_shapes=[
            pltpu.VMEM((STEP, max(sampled, edge_total)), bf16),
            pltpu.VMEM((kinds, rows // low * feat, low), bf16),
            pltpu.VMEM((groups, kinds, cap), i32),
            pltpu.VMEM((groups, kinds, cap), i32),
            pltpu.VMEM((HALVES, kinds, sampled), i32),
            pltpu.VMEM((HALVES, RELS, edge_total), i32),
            pltpu.VMEM((kinds, side, HALVES, feat, cap), bf16),
            pltpu.VMEM((kinds, HALVES, side, feat, cap), bf16),
            pltpu.VMEM((HALVES, RELS, low, sampled // low * SEEDS), bf16),
            pltpu.VMEM((HALVES, RELS, 8, SEEDS), f32),
            pltpu.VMEM((MATS, feat, SEEDS), f32),
            pltpu.VMEM((HALVES, MATS, feat, SEEDS), bf16),
            pltpu.VMEM((HALVES, MATS, feat, SEEDS), bf16),
            pltpu.VMEM((shares, kinds, SEEDS, width), f32),
            pltpu.VMEM((shares, kinds, SEEDS, width), bf16),
            pltpu.VMEM((shares, kinds, SEEDS, width), bf16),
            dma((groups,)), dma((groups,)),
            dma((HALVES, 2)), dma((HALVES, 2)),
            dma((kinds, side, HALVES)), dma((kinds, side, HALVES)),
            dma((HALVES, kinds)), dma((HALVES, kinds)),
            dma((shares,)), dma((shares,)),
        ],
        compiler_params=pltpu.CompilerParams(
            collective_id=0, has_side_effects=True, vmem_limit_bytes=56 * 1024 * 1024),
    )(features, weights, sample_owner[:, :, 0], sample_row, edge_src, edge_dst, edge_count)


def solution(mesh):
    return jax.shard_map(
        per_device,
        mesh=mesh,
        in_specs=(
            P(None, "mp", "dp"),
            P(None, "mp", None),
            P(None, "dp", None),
            P(None, "dp"),
            P(None, "dp"),
            P(None, "dp"),
            P(None, "dp"),
        ),
        out_specs=P(None, "mp", "dp"),
        check_vma=False,
    )
```

time: 248 us -> 71.9 us (0.29); the launches traced: 245 us -> 71.6 us
  matrix products: 127 us -> 0 us
  Pallas kernels: 0 us -> 67.4 us
  waiting for transfers between devices: 41.7 us -> 0 us
  starting transfers between devices: 31.1 us -> 0 us
  local copies, waits for them, and re-layouts: 19.3 us -> 4.23 us
  between operations: 14 us -> 0.01 us
  other arithmetic: 10.3 us -> 0 us
    dot_general x81 -> x0, matrix products: 127 us -> none  [the longest x68 105 us: one_block(): jnp.dot(table, chosen, preferred_element_type=jnp.float32)]
    pallas_call x0 -> x1, Pallas kernels: none -> 67.4 us  [per_device(): pl.pallas_call(functools.partial(kernel, groups, shares), out_shape=jax.S...]
    all_to_all x6 -> x0, starting transfers between devices: 30.9 us -> none  [the longest x3 15.7 us: serve_kind(): return lax.all_to_all(picked, 'dp', split_axis=1, concat_axis=1, tiled=True)]
    reduce_scatter x1 -> x0, waiting for transfers between devices: 25.8 us -> none  [per_device(): lax.psum_scatter(jnp.stack(partial_sums), 'mp', scatter_dimension=1, tile...]
    all_to_all x6 -> x0, waiting for transfers between devices: 15.8 us -> none  [the longest x3 11.4 us: serve_kind(): return lax.all_to_all(picked, 'dp', split_axis=1, concat_axis=1, tiled=True)]
    another operation x28 -> x0, local copies, waits for them, and re-layouts: 8.23 us -> none
    select_n x1 -> x0, other arithmetic: 5.06 us -> none  [per_device(): target = jnp.where(live_edge, edge_dst[relation], -1)]
    squeeze x4 -> x0, local copies, waits for them, and re-layouts: 3.27 us -> none  [the longest x3 3.13 us: per_device(): fetched[node_kind]]
  transfers between devices with their start and end apart: 7 -> 0, of which waited for: 3 -> 0; matrix products, arithmetic and copies ran while one was open for 34% -> 0% of each run, Pallas kernels for 0% -> 0%
where the time goes in v1:
time: 71.9 us; the launch traced here: 71.6 us
  Pallas kernels  67.4 us (94%)
  local copies, waits for them, and re-layouts  4.23 us (6%)
    pallas_call x1, Pallas kernels, per_device(): pl.pallas_call(functools.partial(kernel, groups, shares), out_shape=jax.S...  67.4 us
    unnamed x3, local copies, waits for them, and re-layouts  4.23 us

profile of v1, /device:TPU:1, one launch (start us, length us, event | category | flops | bytes accessed | tf_op | source)
XLA Modules:
  0.0 71.6 jit_solution(15468754501878138994)
XLA Ops:
  0.0 1.3 %copy.8.count = s32[8,1]{1,0:T(8,128)} copy(s32[8,1]{0,1:T(1,128)} %param.13) | data formatting | bytes 64 | tf_op args[6]
  1.3 1.4 %copy.11 = s32[3,2048,1]{1,0,2:T(4,128)} copy(s32[3,2048,1]{1,2,0:T(1,128)} %param.9) | data formatting | bytes 49152
  2.7 67.4 %shard_map.73 = bf16[3,128,128]{2,1,0:T(8,128)(2,1)} custom-call(bf16[3,128,2048]{2,1,0:T(8,128)(2,1)} %features.1, bf16[11,128,512]{2,1,0:T(8,128)(2,1)} %weights.1, s32[3,2048]{1,0:T(4,128)} %bitcast.3, s32[3,2048]{1,0:T(4,128)} %row.1, s32[8,2048]{1,0:T(8,128)} %src.1, s32[8,2048]{1,0:T(8,128)} %dst.1, s32[8,1]{1,0:T(8,128)} %copy.8.count), custom_call_target="tpu_custom_call" | custom-call | tf_op jit(solution)/shard_map/pallas_call | solution.py:261
  70.1 1.5 %copy.13 = bf16[3,128,128]{2,1,0:T(8,128)(2,1)} copy(bf16[3,128,128]{2,1,0:T(8,128)(2,1)} %shard_map.73) | data formatting | bytes 196608

commit v2 on v1

--- a/solution.py
+++ b/solution.py
@@ -18,7 +18,9 @@
 )
 ORDER = tuple(m for group in SLOTS for m in group)
 STARTS = tuple(sum(len(group) for group in SLOTS[:k]) for k in range(KINDS))
+RELATIONS = tuple(m for m in ORDER if m < RELS)
 HALVES = 2
+CORES = 2
 STEP = 256
 MESH = pl.DeviceIdType.MESH
 NT = (((1,), (1,)), ((), ()))
@@ -29,15 +31,16 @@
     return n.bit_length() - 1
 
 
-def kernel(groups, shares, features, weights, owner, row, src, dst, count, out,
-           iota, tab, req_send, req_recv, pos, edges, send, recv, adj, deg, part,
+def kernel(groups, shares, features_in, weights_in, owner, row, src, dst, count, out,
+           features, weights, in_sem, iota, tab, req_send, req_recv, pos, edges, send, recv, adj, deg, part,
            part_send, part_recv, typed, typed_send, typed_recv,
-           req_ss, req_rs, idx_ss, idx_rs, row_ss, row_rs, part_ss, part_rs, typed_ss, typed_rs):
+           req_ss, req_rs, idx_ss, idx_rs, row_ss, row_rs, part_ss, part_rs, typed_ss, typed_rs, adj_ss, adj_rs):
     kinds, feat, rows = features.shape
-    sampled = owner.shape[1]
+    sampled = row.shape[1]
     edge_total = src.shape[1]
     cap = req_send.shape[2]
     low = tab.shape[2]
+    share = RELS // CORES
     high = rows // low
     s_high = sampled // low
     side = groups // HALVES
@@ -45,6 +48,7 @@
     m = lax.axis_index("mp")
     half = g // side
     q = lax.rem(g, side)
+    core = lax.rem(m, CORES)
     f32, bf16, i32 = jnp.float32, jnp.bfloat16, jnp.int32
 
     def one_hot(index, size):
@@ -58,6 +62,10 @@
             pieces.append(jnp.where(hit, jnp.ones((), bf16), jnp.zeros((), bf16)))
         return pieces[0] if len(pieces) == 1 else jnp.concatenate(pieces, axis=0)
 
+    load_features = pltpu.make_async_copy(features_in, features, in_sem.at[0])
+    load_weights = pltpu.make_async_copy(weights_in, weights, in_sem.at[1])
+    load_features.start()
+    load_weights.start()
     barrier = pltpu.get_barrier_semaphore()
     for d in range(1, groups):
         pl.semaphore_signal(barrier, inc=1, device_id={"dp": lax.rem(g + d, groups)}, device_id_type=MESH)
@@ -67,28 +75,36 @@
     iota[...] = lax.broadcasted_iota(i32, iota.shape, 0).astype(f32).astype(bf16)
     tri = (lax.broadcasted_iota(i32, (STEP, STEP), 0) <= lax.broadcasted_iota(i32, (STEP, STEP), 1))
     tri = jnp.where(tri, 1.0, 0.0).astype(bf16)
-    for k in range(kinds):
-        owners = owner[k:k + 1, :]
-        hot = jnp.where(lax.broadcasted_iota(i32, (groups, sampled), 0) == owners, 1.0, 0.0)
-        carry = jnp.zeros((groups, 1), f32)
-        ranks = []
-        for base in range(0, sampled, STEP):
-            piece = hot[:, base:base + STEP]
-            upto = jnp.dot(piece.astype(bf16), tri, preferred_element_type=f32) + carry
-            ranks.append(jnp.sum((upto - 1.0) * piece, axis=0, keepdims=True))
-            carry = carry + jnp.sum(piece, axis=1, keepdims=True)
-        rank = jnp.concatenate(ranks, axis=1).astype(i32)
+    hot = jnp.concatenate([
+        jnp.where(lax.broadcasted_iota(i32, (groups, sampled), 0) == owner[k], 1.0, 0.0)
+        for k in range(kinds)], axis=0)
+    lines = kinds * groups
+    pieces = [hot[:, base:base + STEP] for base in range(0, sampled, STEP)]
+    upto = jnp.dot(jnp.concatenate(pieces, axis=0).astype(bf16), tri, preferred_element_type=f32)
+    carry = jnp.zeros((lines, 1), f32)
+    ranks = []
+    for n, piece in enumerate(pieces):
+        here = upto[n * lines:(n + 1) * lines]
+        ranks.append((here + (carry - 1.0)) * piece)
+        carry = carry + here[:, STEP - 1:]
+    ranks = jnp.concatenate(ranks, axis=1)
+    for k in range(kinds):
+        owners = owner[k]
+        mine = hot[k * groups:(k + 1) * groups]
+        rank = jnp.sum(ranks[k * groups:(k + 1) * groups], axis=0, keepdims=True).astype(i32)
         pos[half, k:k + 1, :] = owners * cap + rank
         wanted = row[k:k + 1, :]
-        coarse = hot * (wanted >> 8).astype(f32)
-        fine = hot * (wanted & 255).astype(f32)
+        coarse = mine * (wanted >> 8).astype(f32)
+        fine = mine * (wanted & 255).astype(f32)
         pair = jnp.concatenate([coarse, fine], axis=0).astype(bf16)
         listed = lax.dot_general(pair, one_hot(rank, cap), NT, preferred_element_type=f32)
         listed = (listed[:groups] * 256.0 + listed[groups:]).astype(i32)
         for o in range(groups):
             req_send[o, k:k + 1, :] = listed[o:o + 1]
-    slots = lax.broadcasted_iota(i32, (RELS, edge_total), 1)
-    edges[half] = jnp.where(slots < count[...], dst[...] * sampled + src[...], -1)
+    slots = lax.broadcasted_iota(i32, (1, edge_total), 1)
+    for n, r in enumerate(RELATIONS):
+        edges[half, n:n + 1, :] = jnp.where(
+            slots < count[0, r], dst[r:r + 1, :] * sampled + src[r:r + 1, :], -1)
 
     pl.semaphore_wait(barrier, groups - 1 + shares - 1)
     asks = []
@@ -109,6 +125,7 @@
             copy.start()
             hints.append(copy)
 
+    load_features.wait()
     for k in range(kinds):
         for h in range(high):
             tab[k, h * feat:(h + 1) * feat, :] = features[k, :, h * low:(h + 1) * low]
@@ -124,7 +141,8 @@
             column = (source >> log2(low)) * SEEDS + (packed >> log2(sampled))
             right = one_hot(jnp.where(live, column, -1), s_high * SEEDS)
             counts = lax.dot_general(left, right, NT, preferred_element_type=f32)
-            adj[i, r] = counts.astype(bf16)
+            for h in range(s_high):
+                adj[i, r, h * low:(h + 1) * low, :] = counts[:, h * SEEDS:(h + 1) * SEEDS].astype(bf16)
             total = jnp.sum(counts, axis=0, keepdims=True)
             seen = total[:, :SEEDS]
             for h in range(1, s_high):
@@ -132,9 +150,19 @@
             deg[i, r] = jnp.broadcast_to(jnp.maximum(seen, 1.0), (8, SEEDS))
             return 0
 
-        lax.fori_loop(lo_r, hi_r, one, 0)
-
-    build(0, 0, 2)
+        lax.fori_loop(core * share + lo_r, core * share + hi_r, one, 0)
+
+    def share_block(i):
+        built = pl.ds(core * share, share)
+        copies = []
+        for n, ref in enumerate((adj, deg)):
+            copies.append(pltpu.make_async_remote_copy(
+                ref.at[i, built], ref.at[i, built], adj_ss.at[i, n], adj_rs.at[i, n],
+                device_id={"mp": m - core + lax.rem(core + 1, CORES)}, device_id_type=MESH))
+            copies[-1].start()
+        return copies
+
+    build(0, 0, 1)
     req_recv[g] = req_send[g]
     for copy in asks:
         copy.wait()
@@ -155,7 +183,7 @@
 
     for k in range(kinds):
         def serve(n, _, k=k):
-            d, j = 1 + n // HALVES, lax.rem(n, HALVES)
+            d, j = 1 + lax.rem(n, side - 1), lax.rem(half + 1 + n // (side - 1), HALVES)
             send[k, d, j] = pick(k, j * side + lax.rem(q + d, side))
             row_copy(k, d, j).start()
             return 0
@@ -168,25 +196,43 @@
 
         lax.fori_loop(0, HALVES, keep, 0)
 
-    build(0, 2, RELS)
+    build(0, 1, share)
+    shared = share_block(0)
     for copy in hints:
         copy.wait()
     for i in range(1, HALVES):
-        build(i, 0, RELS)
-
-    replies = []
+        build(i, 0, share)
+        shared += share_block(i)
+    for copy in shared:
+        copy.wait()
+
+    replies = [[] for _ in range(kinds)]
+    sums = [None] * kinds
+
+    def finish(k):
+        for copy in replies[k]:
+            copy.wait()
+        for n, matrix in enumerate(SLOTS[k]):
+            message = part[STARTS[k] + n]
+            for i in range(1, HALVES):
+                message = message + part_recv[i, STARTS[k] + n].astype(f32)
+            term = lax.dot_general(message.astype(bf16), weights[matrix], TN, preferred_element_type=f32)
+            t = MATRIX_TARGET[matrix]
+            sums[t] = term if sums[t] is None else sums[t] + term
+
     for k in range(kinds):
         start, size = STARTS[k], len(SLOTS[k])
-
-        def landed(n, _, k=k):
-            row_copy(k, 1 + n // HALVES, lax.rem(n, HALVES)).wait()
-            return 0
-
-        lax.fori_loop(0, (side - 1) * HALVES, landed, 0)
+        first = start - k
         for i in reversed(range(HALVES)):
             block = lax.rem(half + i, HALVES)
-            sums = [jnp.zeros((feat, SEEDS), f32) for _ in SLOTS[k][:-1]]
+
+            def landed(n, _, k=k, block=block):
+                row_copy(k, 1 + n, block).wait()
+                return 0
+
+            lax.fori_loop(0, side - 1, landed, 0)
             stack = recv[k, block].reshape(side * feat, cap)
+            gathered = []
             for h in range(s_high):
                 where = pos[block, k:k + 1, h * low:(h + 1) * low]
                 found = jnp.dot(stack, one_hot(where & (cap - 1), cap), preferred_element_type=f32)
@@ -194,13 +240,12 @@
                 chosen = jnp.zeros((feat, low), f32)
                 for o in range(side):
                     chosen = jnp.where(holder == o, found[o * feat:(o + 1) * feat], chosen)
-                chosen = chosen.astype(bf16)
-                if h == 0:
-                    own = chosen[:, :SEEDS].astype(f32)
-                for n, r in enumerate(SLOTS[k][:-1]):
-                    sums[n] = sums[n] + jnp.dot(
-                        chosen, adj[i, r, :, h * SEEDS:(h + 1) * SEEDS], preferred_element_type=f32)
-            values = [value / deg[i, r][:1] for value, r in zip(sums, SLOTS[k][:-1])] + [own]
+                gathered.append(chosen.astype(bf16))
+            gathered = jnp.concatenate(gathered, axis=1)
+            counts = jnp.concatenate([adj[i, first + n] for n in range(size - 1)], axis=1)
+            summed = jnp.dot(gathered, counts, preferred_element_type=f32)
+            values = [summed[:, n * SEEDS:(n + 1) * SEEDS] / deg[i, first + n][:1] for n in range(size - 1)]
+            values.append(gathered[:, :SEEDS].astype(f32))
             for n, value in enumerate(values):
                 if i == 0:
                     part[start + n] = value
@@ -212,18 +257,12 @@
                     part_ss.at[i, k], part_rs.at[i, k],
                     device_id={"dp": block * side + q}, device_id_type=MESH)
                 copy.start()
-                replies.append(copy)
-    for copy in replies:
-        copy.wait()
-
-    sums = [jnp.zeros((SEEDS, weights.shape[2]), f32) for _ in range(kinds)]
-    for n, matrix in enumerate(ORDER):
-        message = part[n]
-        for i in range(1, HALVES):
-            message = message + part_recv[i, n].astype(f32)
-        target = MATRIX_TARGET[matrix]
-        sums[target] = sums[target] + lax.dot_general(
-            message.astype(bf16), weights[matrix], TN, preferred_element_type=f32)
+                replies[k].append(copy)
+        if k == 0:
+            load_weights.wait()
+        else:
+            finish(k - 1)
+    finish(kinds - 1)
     width = typed.shape[3]
     for t in range(kinds):
         for p in range(shares):
@@ -257,13 +296,17 @@
     width = weights.shape[2] // shares
     bf16, f32, i32 = jnp.bfloat16, jnp.float32, jnp.int32
     vmem = pl.BlockSpec(memory_space=pltpu.VMEM)
+    any_space = pl.BlockSpec(memory_space=pl.ANY)
     dma = pltpu.SemaphoreType.DMA
     return pl.pallas_call(
         functools.partial(kernel, groups, shares),
         out_shape=jax.ShapeDtypeStruct((kinds, width, SEEDS), bf16),
-        in_specs=[vmem] * 7,
+        in_specs=[any_space] * 2 + [vmem] * 4 + [pl.BlockSpec(memory_space=pltpu.SMEM)],
         out_specs=vmem,
         scratch_shapes=[
+            pltpu.VMEM(features.shape, bf16),
+            pltpu.VMEM(weights.shape, bf16),
+            dma((2,)),
             pltpu.VMEM((STEP, max(sampled, edge_total)), bf16),
             pltpu.VMEM((kinds, rows // low * feat, low), bf16),
             pltpu.VMEM((groups, kinds, cap), i32),
@@ -272,7 +315,7 @@
             pltpu.VMEM((HALVES, RELS, edge_total), i32),
             pltpu.VMEM((kinds, side, HALVES, feat, cap), bf16),
             pltpu.VMEM((kinds, HALVES, side, feat, cap), bf16),
-            pltpu.VMEM((HALVES, RELS, low, sampled // low * SEEDS), bf16),
+            pltpu.VMEM((HALVES, RELS, sampled, SEEDS), bf16),
             pltpu.VMEM((HALVES, RELS, 8, SEEDS), f32),
             pltpu.VMEM((MATS, feat, SEEDS), f32),
             pltpu.VMEM((HALVES, MATS, feat, SEEDS), bf16),
@@ -285,10 +328,11 @@
             dma((kinds, side, HALVES)), dma((kinds, side, HALVES)),
             dma((HALVES, kinds)), dma((HALVES, kinds)),
             dma((shares,)), dma((shares,)),
+            dma((HALVES, 2)), dma((HALVES, 2)),
         ],
         compiler_params=pltpu.CompilerParams(
             collective_id=0, has_side_effects=True, vmem_limit_bytes=56 * 1024 * 1024),
-    )(features, weights, sample_owner[:, :, 0], sample_row, edge_src, edge_dst, edge_count)
+    )(features, weights, sample_owner.transpose(0, 2, 1), sample_row, edge_src, edge_dst, edge_count.T)
 
 
 def solution(mesh):

time: 71.9 us -> 65.4 us (0.910)
  Pallas kernels: 67.4 us -> 63.7 us
  local copies, waits for them, and re-layouts: 4.23 us -> 1.54 us
    pallas_call x1, Pallas kernels: 67.4 us -> 63.7 us  [per_device(): pl.pallas_call(functools.partial(kernel, groups, shares), out_shape=jax.S...]
    unnamed x3 -> x1, local copies, waits for them, and re-layouts: 4.23 us -> 1.54 us
where the time goes in v2:
time: 65.4 us; the launch traced here: 65.3 us
  Pallas kernels  63.7 us (97%)
  local copies, waits for them, and re-layouts  1.54 us (2%)
    pallas_call x1, Pallas kernels, per_device(): pl.pallas_call(functools.partial(kernel, groups, shares), out_shape=jax.S...  63.7 us
    unnamed x1, local copies, waits for them, and re-layouts  1.54 us

profile of v2, /device:TPU:1, one launch (start us, length us, event | category | flops | bytes accessed | tf_op | source)
XLA Modules:
  0.0 65.3 jit_solution(1590031040909671249)
XLA Ops:
  0.0 63.7 %shard_map.73 = bf16[3,128,128]{2,1,0:T(8,128)(2,1)} custom-call(bf16[3,128,2048]{2,1,0:T(8,128)(2,1)} %features_in.1, bf16[11,128,512]{2,1,0:T(8,128)(2,1)} %weights_in.1, s32[3,1,2048]{2,1,0:T(1,128)} %bitcast.2, s32[3,2048]{1,0:T(4,128)} %row.1, s32[8,2048]{1,0:T(8,128)} %src.1, s32[8,2048]{1,0:T(8,128)} %dst.1, s32[1,8]{1,0:T(1,128)} %bitcast.3), custom_call_target="tpu_custom_call" | custom-call | tf_op jit(solution)/shard_map/pallas_call | solution.py:301
  63.7 1.5 %copy.9 = bf16[3,128,128]{2,1,0:T(8,128)(2,1)} copy(bf16[3,128,128]{2,1,0:T(8,128)(2,1)} %shard_map.73) | data formatting | bytes 196608

commit v3 on v2

--- a/solution.py
+++ b/solution.py
@@ -115,20 +115,16 @@
             device_id={"dp": to}, device_id_type=MESH)
         copy.start()
         asks.append(copy)
-    hints = []
-    for i in range(1, HALVES):
-        to = lax.rem(half + i, HALVES) * side + q
-        for n, ref in enumerate((pos, edges)):
-            copy = pltpu.make_async_remote_copy(
-                ref.at[half], ref.at[half], idx_ss.at[i, n], idx_rs.at[i, n],
-                device_id={"dp": to}, device_id_type=MESH)
-            copy.start()
-            hints.append(copy)
-
     load_features.wait()
     for k in range(kinds):
         for h in range(high):
             tab[k, h * feat:(h + 1) * feat, :] = features[k, :, h * low:(h + 1) * low]
+
+    def unit_copy(i, r, n):
+        ref = (adj, deg)[n]
+        return pltpu.make_async_remote_copy(
+            ref.at[i, r], ref.at[i, r], adj_ss.at[i, lax.rem(r, share), n], adj_rs.at[i, lax.rem(r, share), n],
+            device_id={"mp": m - core + lax.rem(core + 1, CORES)}, device_id_type=MESH)
 
     def build(i, lo_r, hi_r):
         block = lax.rem(half + i, HALVES)
@@ -148,24 +144,26 @@
             for h in range(1, s_high):
                 seen = seen + total[:, h * SEEDS:(h + 1) * SEEDS]
             deg[i, r] = jnp.broadcast_to(jnp.maximum(seen, 1.0), (8, SEEDS))
+            for n in range(2):
+                unit_copy(i, r, n).start()
             return 0
 
         lax.fori_loop(core * share + lo_r, core * share + hi_r, one, 0)
-
-    def share_block(i):
-        built = pl.ds(core * share, share)
-        copies = []
-        for n, ref in enumerate((adj, deg)):
-            copies.append(pltpu.make_async_remote_copy(
-                ref.at[i, built], ref.at[i, built], adj_ss.at[i, n], adj_rs.at[i, n],
-                device_id={"mp": m - core + lax.rem(core + 1, CORES)}, device_id_type=MESH))
-            copies[-1].start()
-        return copies
 
     build(0, 0, 1)
     req_recv[g] = req_send[g]
     for copy in asks:
         copy.wait()
+    hints = []
+    for i in range(1, HALVES):
+        to = lax.rem(half + i, HALVES) * side + q
+        for n, ref in enumerate((pos, edges)):
+            copy = pltpu.make_async_remote_copy(
+                ref.at[half], ref.at[half], idx_ss.at[i, n], idx_rs.at[i, n],
+                device_id={"dp": to}, device_id_type=MESH)
+            copy.start()
+            hints.append(copy)
+
 
     def pick(k, block):
         wanted = req_recv[block, k:k + 1, :]
@@ -197,14 +195,18 @@
         lax.fori_loop(0, HALVES, keep, 0)
 
     build(0, 1, share)
-    shared = share_block(0)
     for copy in hints:
         copy.wait()
     for i in range(1, HALVES):
         build(i, 0, share)
-        shared += share_block(i)
-    for copy in shared:
-        copy.wait()
+
+    def arrived(r, _):
+        for i in range(HALVES):
+            for n in range(2):
+                unit_copy(i, core * share + r, n).wait()
+        return 0
+
+    lax.fori_loop(0, share, arrived, 0)
 
     replies = [[] for _ in range(kinds)]
     sums = [None] * kinds
@@ -328,7 +330,7 @@
             dma((kinds, side, HALVES)), dma((kinds, side, HALVES)),
             dma((HALVES, kinds)), dma((HALVES, kinds)),
             dma((shares,)), dma((shares,)),
-            dma((HALVES, 2)), dma((HALVES, 2)),
+            dma((HALVES, RELS // CORES, 2)), dma((HALVES, RELS // CORES, 2)),
         ],
         compiler_params=pltpu.CompilerParams(
             collective_id=0, has_side_effects=True, vmem_limit_bytes=56 * 1024 * 1024),

time: 65.4 us -> 66.7 us (1.020)
  Pallas kernels: 63.7 us -> 65 us
    pallas_call x1, Pallas kernels: 63.7 us -> 65 us  [per_device(): pl.pallas_call(functools.partial(kernel, groups, shares), out_shape=jax.S...]
where the time goes in v3:
time: 66.7 us; the launch traced here: 66.6 us
  Pallas kernels  65 us (97%)
  local copies, waits for them, and re-layouts  1.54 us (2%)
    pallas_call x1, Pallas kernels, per_device(): pl.pallas_call(functools.partial(kernel, groups, shares), out_shape=jax.S...  65 us
    unnamed x1, local copies, waits for them, and re-layouts  1.54 us

profile of v3, /device:TPU:1, one launch (start us, length us, event | category | flops | bytes accessed | tf_op | source)
XLA Modules:
  0.0 66.6 jit_solution(3818794905011867287)
XLA Ops:
  0.0 65.0 %shard_map.73 = bf16[3,128,128]{2,1,0:T(8,128)(2,1)} custom-call(bf16[3,128,2048]{2,1,0:T(8,128)(2,1)} %features_in.1, bf16[11,128,512]{2,1,0:T(8,128)(2,1)} %weights_in.1, s32[3,1,2048]{2,1,0:T(1,128)} %bitcast.2, s32[3,2048]{1,0:T(4,128)} %row.1, s32[8,2048]{1,0:T(8,128)} %src.1, s32[8,2048]{1,0:T(8,128)} %dst.1, s32[1,8]{1,0:T(1,128)} %bitcast.3), custom_call_target="tpu_custom_call" | custom-call | tf_op jit(solution)/shard_map/pallas_call | solution.py:303
  65.0 1.5 %copy.9 = bf16[3,128,128]{2,1,0:T(8,128)(2,1)} copy(bf16[3,128,128]{2,1,0:T(8,128)(2,1)} %shard_map.73) | data formatting | bytes 196608

commit v4 on v3

--- a/solution.py
+++ b/solution.py
@@ -115,6 +115,16 @@
             device_id={"dp": to}, device_id_type=MESH)
         copy.start()
         asks.append(copy)
+    hints = []
+    for i in range(1, HALVES):
+        to = lax.rem(half + i, HALVES) * side + q
+        for n, ref in enumerate((pos, edges)):
+            copy = pltpu.make_async_remote_copy(
+                ref.at[half], ref.at[half], idx_ss.at[i, n], idx_rs.at[i, n],
+                device_id={"dp": to}, device_id_type=MESH)
+            copy.start()
+            hints.append(copy)
+
     load_features.wait()
     for k in range(kinds):
         for h in range(high):
@@ -154,16 +164,6 @@
     req_recv[g] = req_send[g]
     for copy in asks:
         copy.wait()
-    hints = []
-    for i in range(1, HALVES):
-        to = lax.rem(half + i, HALVES) * side + q
-        for n, ref in enumerate((pos, edges)):
-            copy = pltpu.make_async_remote_copy(
-                ref.at[half], ref.at[half], idx_ss.at[i, n], idx_rs.at[i, n],
-                device_id={"dp": to}, device_id_type=MESH)
-            copy.start()
-            hints.append(copy)
-
 
     def pick(k, block):
         wanted = req_recv[block, k:k + 1, :]

time: 66.7 us -> 65.7 us (0.985)
  Pallas kernels: 65 us -> 63.9 us
    pallas_call x1, Pallas kernels: 65 us -> 63.9 us  [per_device(): pl.pallas_call(functools.partial(kernel, groups, shares), out_shape=jax.S...]
where the time goes in v4:
time: 65.7 us; the launch traced here: 65.5 us
  Pallas kernels  63.9 us (97%)
  local copies, waits for them, and re-layouts  1.54 us (2%)
    pallas_call x1, Pallas kernels, per_device(): pl.pallas_call(functools.partial(kernel, groups, shares), out_shape=jax.S...  63.9 us
    unnamed x1, local copies, waits for them, and re-layouts  1.54 us

profile of v4, /device:TPU:1, one launch (start us, length us, event | category | flops | bytes accessed | tf_op | source)
XLA Modules:
  0.0 65.5 jit_solution(1685937587277327835)
XLA Ops:
  0.0 63.9 %shard_map.73 = bf16[3,128,128]{2,1,0:T(8,128)(2,1)} custom-call(bf16[3,128,2048]{2,1,0:T(8,128)(2,1)} %features_in.1, bf16[11,128,512]{2,1,0:T(8,128)(2,1)} %weights_in.1, s32[3,1,2048]{2,1,0:T(1,128)} %bitcast.2, s32[3,2048]{1,0:T(4,128)} %row.1, s32[8,2048]{1,0:T(8,128)} %src.1, s32[8,2048]{1,0:T(8,128)} %dst.1, s32[1,8]{1,0:T(1,128)} %bitcast.3), custom_call_target="tpu_custom_call" | custom-call | tf_op jit(solution)/shard_map/pallas_call | solution.py:303
  63.9 1.5 %copy.9 = bf16[3,128,128]{2,1,0:T(8,128)(2,1)} copy(bf16[3,128,128]{2,1,0:T(8,128)(2,1)} %shard_map.73) | data formatting | bytes 196608
